TPU v7x, 512 devices: a 8x2x16 block of a 8x8x16 slice. The times are simulated.
512 devices in a mesh: grp: 2 (over y), col: 16 (over z), slc: 8 (over x), bat: 2 (over core).
Axes of the slice: x: 8, y: 2, z: 16, core: 2. Of those that a mesh axis runs over, the one named last changes fastest.
The devices are a block of a 8x8x16 slice.
Arguments:
- site_tensors: bfloat16 [16, 288, 2, 64, 128], P(('grp', 'slc'), 'col'), parts along dimension 0, may hold values from -1.2 to 1.2
- left_edge: float32 [16, 64, 128], P(('grp', 'slc')), parts along dimension 0, may hold values from -0.5 to 0.5
- right_edge: float32 [16, 64, 128], P(('grp', 'slc')), parts along dimension 0, may hold values from -0.5 to 0.5
- order: int32 [576], P(('grp', 'col')), parts along dimension 0, may hold values from 0 to 287, each once
- bitstrings: int32 [128, 288], P(('grp', 'bat')), parts along dimension 0, may hold values 0 or 1
Outputs:
- amplitudes: float32 [2, 128], P(None, ('grp', 'bat')), parts along dimension 1
There are 2 independent parts, one for each index of `grp`. A program takes and returns all parts, laid end to end along the dimension named above; each array names one. Nothing has to cross between parts.
Inputs may be any that keep to these rules, and one draw needn't show every extreme that they name: `order`: a permutation of the 288 qubit indices.
All inputs are finite; a program needn't handle non-finite values. No bound on the sum of `bitstrings` on one device may be relied on, other than what follows from the above.
Results may differ from a plain program's by a relative error of at most 0.0003.
Values sent between devices are 32-bit elements; how exact they have to be, the bound alone decides.
No kernel may reach another device: no remote copies, remote signals or barrier semaphores. Data moves between devices by JAX's collectives and lax.ppermute only.
A program may use at most 64 MiB of HBM per device.

v0:
```python
import functools

import jax
import jax.numpy as jnp
from jax import lax
from jax.experimental import pallas as pl
from jax.experimental.pallas import tpu as pltpu
from jax.sharding import Mesh, PartitionSpec as P


F32 = jnp.float32
BF16 = jnp.bfloat16
BLOCK = 4
PREFIX = 4
SHIFT = 1
PARAMS = pltpu.CompilerParams(vmem_limit_bytes=16 * 1024 * 1024)


def lane_sign(rows, width):
    lane = lax.broadcasted_iota(jnp.int32, (rows, width), 1)
    return jnp.where(lane < width // 2, -1.0, 1.0).astype(F32)


def rotated(block, sign):
    return pltpu.roll(block, block.shape[1] // 2, 1) * sign


def split(value):
    high = value.astype(BF16)
    low = (value - high.astype(F32)).astype(BF16)
    return high, low


def dot(a, b):
    return jnp.dot(a, b, preferred_element_type=F32)


def pair_product(first, second, sign):
    width = first.shape[1]
    first_high, first_low = split(first)
    second_high, second_low = split(jnp.concatenate([second, rotated(second, sign)], axis=0))
    half = jnp.concatenate([second_high, second_low], axis=1)
    both = dot(
        jnp.concatenate([first_high, first_low], axis=1),
        jnp.concatenate([half, half], axis=0),
    )
    return both[:, :width] + both[:, width:]


def opening_matrix(left, right, sign):
    bond, _ = left.shape
    left_high, left_low = split(left)
    right_high, right_low = split(right)
    gram = lax.dot_general(
        jnp.concatenate([right_high, right_high, right_low, right_low], axis=0),
        jnp.concatenate([left_high, left_low, left_high, left_low], axis=0),
        (((0,), (0,)), ((), ())),
        preferred_element_type=F32,
    )
    return gram[:bond] + rotated(gram[bond:], sign)


def column_kernel(
    base, order_ref, role_ref, bits_hbm, tensors_hbm, left_hbm, right_hbm, out_ref,
    bits_ref, tensors_ref, left_ref, right_ref, state_ref, table_ref, start_ref, word_ref, words_ref, arrived,
):
    sites, _, bond, width = tensors_ref.shape
    slots = out_ref.shape[0]
    copies = [
        pltpu.make_async_copy(source, target, arrived.at[index])
        for index, (source, target) in enumerate(
            (
                (bits_hbm, bits_ref),
                (tensors_hbm.at[pl.ds(0, PREFIX)], tensors_ref.at[pl.ds(0, PREFIX)]),
                (tensors_hbm.at[pl.ds(PREFIX, sites - PREFIX)], tensors_ref.at[pl.ds(PREFIX, sites - PREFIX)]),
            )
        )
    ]
    for copy in copies:
        copy.start()
    sign = lane_sign(bond, width)
    mask = role_ref[0]
    qubit = lax.broadcasted_iota(jnp.int32, (8, bits_ref.shape[1]), 1)
    place = jnp.zeros(qubit.shape, F32)
    for site in range(sites):
        place = jnp.where(qubit == order_ref[site], float(1 << site), place)
    place = place.astype(BF16)

    def weights(site):
        halves = []
        for value in range(2):
            tensor = tensors_ref[site, value].astype(F32)
            halves.append(jnp.concatenate([tensor, rotated(tensor, sign)], axis=0).astype(BF16))
        half = jnp.concatenate(halves, axis=1)
        return jnp.concatenate([half, half], axis=0)

    copies[0].wait()
    word = lax.dot_general(
        place, bits_ref[...].astype(F32).astype(BF16), (((1,), (1,)), ((), ())), preferred_element_type=F32
    )
    word_ref[...] = jnp.zeros(word_ref.shape, jnp.int32)
    word_ref[:, :word.shape[1]] = word.astype(jnp.int32)
    to_scalars = pltpu.make_async_copy(word_ref, words_ref, arrived.at[len(copies)])
    to_scalars.start()

    copies[1].wait()
    for value in range(2):
        start_ref[value * bond:(value + 1) * bond, :width] = tensors_ref[0, value]
    start_ref[:, width:] = jnp.zeros((2 * bond, width), BF16)

    @pl.when(role_ref[1] == 1)
    def _():
        edges = [
            pltpu.make_async_copy(left_hbm, left_ref, arrived.at[len(copies) + 1]),
            pltpu.make_async_copy(right_hbm, right_ref, arrived.at[len(copies) + 2]),
        ]
        for edge in edges:
            edge.start()
        for edge in edges:
            edge.wait()
        high, low = split(opening_matrix(left_ref[...], right_ref[...], sign))
        both = dot(jnp.concatenate([high, low], axis=1), weights(0))
        high, low = split(jnp.concatenate([both[:, :width], both[:, width:]], axis=0))
        start_ref[:, :width] = high
        start_ref[:, width:] = low

    operand = start_ref[...]
    for site in range(1, PREFIX):
        both = dot(operand, weights(site))
        high, low = split(jnp.concatenate([both[:, :width], both[:, width:]], axis=0))
        operand = jnp.concatenate([high, low], axis=1)
    table_ref[...] = operand
    to_scalars.wait()
    words = [words_ref[0, (base + slot) ^ mask] for slot in range(slots)]
    for slot in range(slots):
        start = pl.multiple_of((words[slot] & ((1 << PREFIX) - 1)) * bond, bond)
        state_ref[slot * bond:(slot + 1) * bond, :] = table_ref[pl.ds(start, bond), :]

    copies[2].wait()
    for site in range(PREFIX, sites):
        matrix = weights(site)
        for start in range(0, slots, BLOCK):
            both = dot(state_ref[start * bond:(start + BLOCK) * bond, :], matrix)
            for slot in range(start, start + BLOCK):
                part = both[(slot - start) * bond:(slot - start + 1) * bond]
                value = jnp.where((words[slot] & (1 << site)) != 0, part[:, width:], part[:, :width])
                if site == sites - 1:
                    out_ref[slot] = value
                else:
                    high, low = split(value)
                    state_ref[slot * bond:(slot + 1) * bond, :width] = high
                    state_ref[slot * bond:(slot + 1) * bond, width:] = low


def column_products(base, slots, order, bits, role, tensors, left, right):
    sites, _, bond, width = tensors.shape
    scalar = pl.BlockSpec(memory_space=pltpu.SMEM)
    far = pl.BlockSpec(memory_space=pltpu.HBM)
    return pl.pallas_call(
        functools.partial(column_kernel, base),
        out_shape=jax.ShapeDtypeStruct((slots, bond, width), F32),
        in_specs=[scalar, scalar, far, far, far, far],
        out_specs=pl.BlockSpec(memory_space=pltpu.VMEM),
        scratch_shapes=[
            pltpu.VMEM(bits.shape, jnp.int32),
            pltpu.VMEM(tensors.shape, BF16),
            pltpu.VMEM((bond, width), F32),
            pltpu.VMEM((bond, width), F32),
            pltpu.VMEM((slots * bond, 2 * width), BF16),
            pltpu.VMEM(((1 << PREFIX) * bond, 2 * width), BF16),
            pltpu.VMEM((2 * bond, 2 * width), BF16),
            pltpu.VMEM((8, width), jnp.int32),
            pltpu.SMEM((8, width), jnp.int32),
            pltpu.SemaphoreType.DMA((6,)),
        ],
        cost_estimate=pl.CostEstimate(
            flops=sites * slots * bond * (2 * width) ** 2, bytes_accessed=slots * bond * width * 8, transcendentals=0
        ),
        compiler_params=PARAMS,
        name="column_products",
    )(order, role, *(pltpu.with_memory_space_constraint(a, pltpu.HBM) for a in (bits, tensors, left, right)))


def joined(flag, kept, received, sign):
    before = jnp.where(flag, received, kept)
    after = jnp.where(flag, kept, received)
    return pair_product(before, after, sign)


def join_kernel(role_ref, kept_ref, received_ref, *out_refs):
    items, bond, width = kept_ref.shape
    sign = lane_sign(bond, width)
    flag = role_ref[0] == 1
    per = out_refs[0].shape[0]
    for item in range(items):
        out_refs[item // per][item % per] = joined(flag, kept_ref[item], received_ref[item], sign)


def join(flag, kept, received, outs):
    items, bond, width = kept.shape
    out = jax.ShapeDtypeStruct((items // outs, bond, width), F32)
    vector = pl.BlockSpec(memory_space=pltpu.VMEM)
    return pl.pallas_call(
        join_kernel,
        out_shape=(out,) * outs,
        in_specs=[pl.BlockSpec(memory_space=pltpu.SMEM), vector, vector],
        out_specs=(vector,) * outs,
        compiler_params=PARAMS,
        name="join",
    )(flag, kept, received)


def close_kernel(role_ref, opened_ref, kept_ref, received_ref, out_ref):
    items, bond, width = kept_ref.shape
    sign = lane_sign(bond, width)
    row = lax.broadcasted_iota(jnp.int32, (bond, width), 0)
    lane = lax.broadcasted_iota(jnp.int32, (bond, width), 1)
    slot = lax.broadcasted_iota(jnp.int32, out_ref.shape, 1)
    which = lax.broadcasted_iota(jnp.int32, out_ref.shape, 0)
    flag = role_ref[1] == 1
    late = role_ref[2] == 1
    total = jnp.zeros(out_ref.shape, F32)
    for item in range(items):
        end = joined(flag, kept_ref[item], received_ref[item], sign)
        whole = pair_product(opened_ref[item], end, sign)
        real = jnp.sum(jnp.where(row == lane, whole, 0.0), keepdims=True)
        imag = jnp.sum(jnp.where(row + bond == lane, whole, 0.0), keepdims=True)
        value = jnp.where(which == 0, real, imag)
        total = jnp.where(slot == (role_ref[0] ^ item), value, total)
    out_ref[...] = jnp.where(late, total, 0.0)


def close(base, opened, kept, received, rows):
    vector = pl.BlockSpec(memory_space=pltpu.VMEM)
    return pl.pallas_call(
        close_kernel,
        out_shape=jax.ShapeDtypeStruct((2, rows), F32),
        in_specs=[pl.BlockSpec(memory_space=pltpu.SMEM), vector, vector, vector],
        out_specs=vector,
        compiler_params=PARAMS,
        name="close",
    )(base, opened, kept, received)


AXES = ("far", "near", "bat")


def pairs(cols, cores, target):
    found = []
    for core in range(cores):
        for role in range(cols):
            other = target(role)
            if other is not None:
                found.append(((role + SHIFT * core) % cols * cores + core, (other + SHIFT * core) % cols * cores + core))
    return found


def solution(mesh):
    shape = dict(mesh.shape)
    inner = 4
    outer = shape["col"] // inner
    cores = shape["bat"]
    cols = shape["col"]
    half, quarter = cols // 2, cols // 4
    fine = Mesh(
        mesh.devices.reshape(shape["grp"], outer, inner, shape["slc"], cores),
        ("grp", "far", "near", "slc", "bat"),
    )

    def swap(distance, late):
        return pairs(cols, cores, lambda role: role ^ distance if (role >= half) == late else None)

    def on_device(site_tensors, left_edge, right_edge, order, bitstrings):
        rows = bitstrings.shape[0]
        core = lax.axis_index("bat")
        col = lax.axis_index("far") * inner + lax.axis_index("near")
        role = (col - SHIFT * core + cols) % cols
        bit0, bit1, bit2, late = role & 1, (role >> 1) & 1, (role >> 2) & 1, (role >> 3) & 1
        mask = bit0 * (rows // 2) + bit1 * (rows // 4) + (bit2 ^ late) * (rows // 8)
        first = (col == 0).astype(jnp.int32)
        operands = (order, bitstrings, jnp.stack([mask, first]), site_tensors[0], left_edge[0], right_edge[0])
        sent = column_products(rows // 2, rows // 2, *operands)
        kept = column_products(0, rows // 2, *operands)

        def move(value, found):
            return lax.ppermute(value, AXES, found)

        def quads(late):
            received = move(sent, swap(1, late))
            stay, leave = join(bit0[None], kept, received, 2)
            received = move(leave, swap(2, late))
            return join(bit1[None], stay, received, 2)

        stay, leave = quads(False)
        received = move(leave, swap(quarter, False))
        (early,) = join(bit2[None], stay, received, 1)
        across = pairs(cols, cores, lambda role: (role ^ quarter) + half if role < half else None)
        opened = move(early, across)
        stay, leave = quads(True)
        received = move(leave, swap(quarter, True))
        placed = close(jnp.stack([mask, bit2, late]), opened, stay, received, rows)
        everyone = outer * inner * shape["slc"]
        spread = jnp.broadcast_to(placed, (everyone, 2, rows))
        gathered = lax.all_to_all(spread, ("far", "near", "slc"), split_axis=0, concat_axis=0, tiled=True)
        return jnp.sum(gathered, axis=0)

    return jax.shard_map(
        on_device,
        mesh=fine,
        in_specs=(
            P(("grp", "slc"), ("far", "near"), None, None, None),
            P(("grp", "slc"), None, None),
            P(("grp", "slc"), None, None),
            P(("grp", "far", "near")),
            P(("grp", "bat"), None),
        ),
        out_specs=P(None, ("grp", "bat")),
        check_vma=False,
    )
```

profile of v0, /device:TPU:80, one launch (start us, length us, event | category | flops | bytes accessed | tf_op | source)
XLA Modules:
  0.0 124.7 jit_solution(1006636069697101478)
XLA Ops:
  0.0 0.1 pad_add_fusion.1.role_ref
  0.1 0.0 copy-start
  0.1 0.7 copy-done
  0.7 5.7 %column_products.3 = f32[16,64,128]{2,1,0:T(8,128)S(1)} custom-call(s32[18]{0:T(128)S(1)} %copy-done, s32[2]{0:T(128)S(1)} %pad_add_fusion.1.role_ref, s32[32,288]{1,0:T(8,128)} %bits_hbm.3, bf16[18,2,64,128]{3,2,1,0:T(8,128)(2,1)} %bitcast.9, f32[64,128]{1,0:T(8,128)} %bitcast.11, f32[64,128]{1,0:T(8,128)} %bitcast.13), custom_call_target="tpu_custom_call" | custom-call | flops 1207959552 | bytes 1048576 | tf_op jit(solution)/shard_map/column_products/pallas_call | solution.py:159
  6.4 4.8 %collective-permute-start = (f32[16,64,128]{2,1,0:T(8,128)S(1)}, f32[16,64,128]{2,1,0:T(8,128)S(1)}, u32[]{:S(2)}, u32[]{:S(2)}) collective-permute-start(f32[16,64,128]{2,1,0:T(8,128)S(1)} %column_products.3), channel_id=1, source_target_pairs={{0,16},{16,0},{32,48},{48,32},{64,80},{80,64},{96,112},{112,96},{1... | collective-permute-start | bytes 1572872 | tf_op jit(solution)/shard_map/ppermute | solution.py:286
  11.3 0.7 collective-permute-start.4
  12.0 5.7 %column_products.2.kept_ref = f32[16,64,128]{2,1,0:T(8,128)S(1)} custom-call(s32[18]{0:T(128)S(1)} %copy-done, s32[2]{0:T(128)S(1)} %pad_add_fusion.1.role_ref, s32[32,288]{1,0:T(8,128)} %bits_hbm.3, bf16[18,2,64,128]{3,2,1,0:T(8,128)(2,1)} %bitcast.10, f32[64,128]{1,0:T(8,128)} %bitcast.12, f32[64,128]{1,0:T(8,128)} %bitcast.14), custom_call_target="tpu_custom_call" | custom-call | flops 1207959552 | bytes 1048576 | tf_op jit(solution)/shard_map/column_products/pallas_call | solution.py:159
  17.7 0.7 collective-permute-done.received_ref
  18.4 0.6 join.5
  19.0 9.6 %collective-permute-start.1 = (f32[8,64,128]{2,1,0:T(8,128)S(1)}, f32[8,64,128]{2,1,0:T(8,128)S(1)}, u32[]{:S(2)}, u32[]{:S(2)}) collective-permute-start(f32[8,64,128]{2,1,0:T(8,128)S(1)} %get-tuple-element.14), channel_id=1, source_target_pairs={{0,32},{16,48},{32,0},{48,16},{64,96},{80,112},{96,64},{112,80},{1... | collective-permute-start | bytes 786440 | tf_op jit(solution)/shard_map/ppermute | solution.py:286
  28.5 0.0 collective-permute-done.4.received_ref
  28.6 0.6 join.8
  29.1 0.7 collective-permute-start.5
  29.8 7.1 %collective-permute-done.1.received_ref = f32[8,64,128]{2,1,0:T(8,128)S(1)} collective-permute-done((f32[8,64,128]{2,1,0:T(8,128)S(1)}, f32[8,64,128]{2,1,0:T(8,128)S(1)}, u32[]{:S(2)}, u32[]{:S(2)}) %collective-permute-start.1) | collective-permute-done | bytes 262176 | tf_op jit(solution)/shard_map/ppermute | solution.py:286
  37.0 0.4 join.6
  37.3 17.8 %collective-permute-start.2 = (f32[4,64,128]{2,1,0:T(8,128)S(1)}, f32[4,64,128]{2,1,0:T(8,128)S(1)}, u32[]{:S(2)}, u32[]{:S(2)}) collective-permute-start(f32[4,64,128]{2,1,0:T(8,128)S(1)} %get-tuple-element.16), channel_id=1, source_target_pairs={{0,64},{16,80},{32,96},{48,112},{64,0},{80,16},{96,32},{112,48},{1... | collective-permute-start | bytes 393224 | tf_op jit(solution)/shard_map/ppermute | solution.py:286
  55.2 0.0 collective-permute-done.5.received_ref
  55.2 0.4 join.9
  55.6 0.7 collective-permute-start.6
  56.2 2.2 %collective-permute-done.2.received_ref = f32[4,64,128]{2,1,0:T(8,128)S(1)} collective-permute-done((f32[4,64,128]{2,1,0:T(8,128)S(1)}, f32[4,64,128]{2,1,0:T(8,128)S(1)}, u32[]{:S(2)}, u32[]{:S(2)}) %collective-permute-start.2) | collective-permute-done | bytes 131104 | tf_op jit(solution)/shard_map/ppermute | solution.py:286
  58.5 0.3 join.7
  58.8 13.9 %collective-permute-start.3 = (f32[4,64,128]{2,1,0:T(8,128)S(1)}, f32[4,64,128]{2,1,0:T(8,128)S(1)}, u32[]{:S(2)}, u32[]{:S(2)}) collective-permute-start(f32[4,64,128]{2,1,0:T(8,128)S(1)} %join.7), channel_id=1, source_target_pairs={{0,192},{16,208},{32,224},{48,240},{64,128},{80,144},{96,160},{112... | collective-permute-start | bytes 393224 | tf_op jit(solution)/shard_map/ppermute | solution.py:286
  72.6 0.1 pad_add_fusion.role_ref
  72.7 0.0 collective-permute-done.6.received_ref
  72.7 2.4 %collective-permute-done.3.opened_ref = f32[4,64,128]{2,1,0:T(8,128)S(1)} collective-permute-done((f32[4,64,128]{2,1,0:T(8,128)S(1)}, f32[4,64,128]{2,1,0:T(8,128)S(1)}, u32[]{:S(2)}, u32[]{:S(2)}) %collective-permute-start.3) | collective-permute-done | bytes 131104 | tf_op jit(solution)/shard_map/ppermute | solution.py:286
  75.1 1.3 %close.1 = f32[2,32]{1,0:T(2,128)S(1)} custom-call(s32[3]{0:T(128)S(1)} %pad_add_fusion.role_ref, f32[4,64,128]{2,1,0:T(8,128)S(1)} %collective-permute-done.3.opened_ref, f32[4,64,128]{2,1,0:T(8,128)S(1)} %get-tuple-element.19.kept_ref, f32[4,64,128]{2,1,0:T(8,128)S(1)} %collective-permute-done.6.received_ref), custom_call_target="tpu_custom_call" | custom-call | tf_op jit(solution)/shard_map/close/pallas_call | solution.py:235
  76.5 47.5 %all_to_all.5 = f32[128,2,32]{2,1,0:T(2,128)S(1)} all-to-all(f32[128,2,32]{2,1,0:T(2,128)S(1)} %broadcast_in_dim.14), channel_id=1, replica_groups=mesh['grp'=2,'far'=4,'near'=4,'slc'=8,'bat'=2] {'far','near','slc'}, dimensions={0} | all-to-all | bytes 65536 | tf_op jit(solution)/shard_map/all_to_all | solution.py:304
  124.0 0.7 reduce_sum.9
  (1 shorter events, 0.0 us)
Async XLA Ops:
  0.1 0.7 copy-start
  6.4 12.0 %collective-permute-start = (f32[16,64,128]{2,1,0:T(8,128)S(1)}, f32[16,64,128]{2,1,0:T(8,128)S(1)}, u32[]{:S(2)}, u32[]{:S(2)}) collective-permute-start(f32[16,64,128]{2,1,0:T(8,128)S(1)} %column_products.3), channel_id=1, source_target_pairs={{0,16},{16,0},{32,48},{48,32},{64,80},{80,64},{96,112},{112,96},{1... | collective-permute-start | bytes 1572872 | tf_op jit(solution)/shard_map/ppermute | solution.py:286
  11.3 17.3 %collective-permute-start.4 = (f32[16,64,128]{2,1,0:T(8,128)S(1)}, f32[16,64,128]{2,1,0:T(8,128)S(1)}, u32[]{:S(2)}, u32[]{:S(2)}) collective-permute-start(f32[16,64,128]{2,1,0:T(8,128)S(1)} %column_products.3), channel_id=1, source_target_pairs={{128,144},{144,128},{160,176},{176,160},{192,208},{208,192},{224,2... | collective-permute-start | bytes 1572872 | tf_op jit(solution)/shard_map/ppermute | solution.py:286
  19.0 18.0 %collective-permute-start.1 = (f32[8,64,128]{2,1,0:T(8,128)S(1)}, f32[8,64,128]{2,1,0:T(8,128)S(1)}, u32[]{:S(2)}, u32[]{:S(2)}) collective-permute-start(f32[8,64,128]{2,1,0:T(8,128)S(1)} %get-tuple-element.14), channel_id=1, source_target_pairs={{0,32},{16,48},{32,0},{48,16},{64,96},{80,112},{96,64},{112,80},{1... | collective-permute-start | bytes 786440 | tf_op jit(solution)/shard_map/ppermute | solution.py:286
  29.1 26.0 %collective-permute-start.5 = (f32[8,64,128]{2,1,0:T(8,128)S(1)}, f32[8,64,128]{2,1,0:T(8,128)S(1)}, u32[]{:S(2)}, u32[]{:S(2)}) collective-permute-start(f32[8,64,128]{2,1,0:T(8,128)S(1)} %get-tuple-element.18), channel_id=1, source_target_pairs={{128,160},{144,176},{160,128},{176,144},{192,224},{208,240},{224,1... | collective-permute-start | bytes 786440 | tf_op jit(solution)/shard_map/ppermute | solution.py:286
  37.3 21.1 %collective-permute-start.2 = (f32[4,64,128]{2,1,0:T(8,128)S(1)}, f32[4,64,128]{2,1,0:T(8,128)S(1)}, u32[]{:S(2)}, u32[]{:S(2)}) collective-permute-start(f32[4,64,128]{2,1,0:T(8,128)S(1)} %get-tuple-element.16), channel_id=1, source_target_pairs={{0,64},{16,80},{32,96},{48,112},{64,0},{80,16},{96,32},{112,48},{1... | collective-permute-start | bytes 393224 | tf_op jit(solution)/shard_map/ppermute | solution.py:286
  55.6 17.2 %collective-permute-start.6 = (f32[4,64,128]{2,1,0:T(8,128)S(1)}, f32[4,64,128]{2,1,0:T(8,128)S(1)}, u32[]{:S(2)}, u32[]{:S(2)}) collective-permute-start(f32[4,64,128]{2,1,0:T(8,128)S(1)} %get-tuple-element.20), channel_id=1, source_target_pairs={{128,192},{144,208},{160,224},{176,240},{192,128},{208,144},{224,1... | collective-permute-start | bytes 393224 | tf_op jit(solution)/shard_map/ppermute | solution.py:286
  58.8 16.4 %collective-permute-start.3 = (f32[4,64,128]{2,1,0:T(8,128)S(1)}, f32[4,64,128]{2,1,0:T(8,128)S(1)}, u32[]{:S(2)}, u32[]{:S(2)}) collective-permute-start(f32[4,64,128]{2,1,0:T(8,128)S(1)} %join.7), channel_id=1, source_target_pairs={{0,192},{16,208},{32,224},{48,240},{64,128},{80,144},{96,160},{112... | collective-permute-start | bytes 393224 | tf_op jit(solution)/shard_map/ppermute | solution.py:286
where the time goes:
time: 125 us
  starting transfers between devices  48.1 us (38%)
  blocking collectives  47.5 us (38%)
  Pallas kernels  14.9 us (12%)
  waiting for transfers between devices  12.5 us (10%)
    ppermute x7, starting transfers between devices, move(): return lax.ppermute(value, AXES, found)  48.1 us
    all_to_all x1, blocking collectives, on_device(): lax.all_to_all(spread, ('far', 'near', 'slc'), split_axis=0, concat_axis=...  47.5 us
    ppermute x7, waiting for transfers between devices, move(): return lax.ppermute(value, AXES, found)  12.5 us
    pallas_call x2, Pallas kernels, column_products(): pl.pallas_call(functools.partial(column_kernel, base), out_shape=jax.Shap...  11.4 us
  transfers between devices with their start and end apart: 7, of which 4 were waited for; matrix products, arithmetic and copies ran while one was open for 0% of the time, Pallas kernels for 6%

commit v1 on v0

--- a/solution.py
+++ b/solution.py
@@ -210,36 +210,33 @@
     )(flag, kept, received)
 
 
-def close_kernel(role_ref, opened_ref, kept_ref, received_ref, out_ref):
-    items, bond, width = kept_ref.shape
+def close_kernel(role_ref, opened_ref, received_ref, out_ref):
+    items, bond, width = received_ref.shape
     sign = lane_sign(bond, width)
     row = lax.broadcasted_iota(jnp.int32, (bond, width), 0)
     lane = lax.broadcasted_iota(jnp.int32, (bond, width), 1)
     slot = lax.broadcasted_iota(jnp.int32, out_ref.shape, 1)
     which = lax.broadcasted_iota(jnp.int32, out_ref.shape, 0)
-    flag = role_ref[1] == 1
-    late = role_ref[2] == 1
     total = jnp.zeros(out_ref.shape, F32)
     for item in range(items):
-        end = joined(flag, kept_ref[item], received_ref[item], sign)
-        whole = pair_product(opened_ref[item], end, sign)
+        whole = pair_product(opened_ref[item], received_ref[item], sign)
         real = jnp.sum(jnp.where(row == lane, whole, 0.0), keepdims=True)
         imag = jnp.sum(jnp.where(row + bond == lane, whole, 0.0), keepdims=True)
         value = jnp.where(which == 0, real, imag)
         total = jnp.where(slot == (role_ref[0] ^ item), value, total)
-    out_ref[...] = jnp.where(late, total, 0.0)
-
-
-def close(base, opened, kept, received, rows):
+    out_ref[...] = jnp.where(role_ref[1] == 1, total, 0.0)
+
+
+def close(base, opened, received, rows):
     vector = pl.BlockSpec(memory_space=pltpu.VMEM)
     return pl.pallas_call(
         close_kernel,
         out_shape=jax.ShapeDtypeStruct((2, rows), F32),
-        in_specs=[pl.BlockSpec(memory_space=pltpu.SMEM), vector, vector, vector],
+        in_specs=[pl.BlockSpec(memory_space=pltpu.SMEM), vector, vector],
         out_specs=vector,
         compiler_params=PARAMS,
         name="close",
-    )(base, opened, kept, received)
+    )(base, opened, received)
 
 
 AXES = ("far", "near", "bat")
@@ -298,7 +295,8 @@
         opened = move(early, across)
         stay, leave = quads(True)
         received = move(leave, swap(quarter, True))
-        placed = close(jnp.stack([mask, bit2, late]), opened, stay, received, rows)
+        (opened,) = join(bit2[None], opened, stay, 1)
+        placed = close(jnp.stack([mask, late]), opened, received, rows)
         everyone = outer * inner * shape["slc"]
         spread = jnp.broadcast_to(placed, (everyone, 2, rows))
         gathered = lax.all_to_all(spread, ("far", "near", "slc"), split_axis=0, concat_axis=0, tiled=True)

time: 125 us -> 121 us (0.968)
  waiting for transfers between devices: 12.5 us -> 21.6 us
  blocking collectives: 47.5 us -> 40.3 us
  starting transfers between devices: 48.1 us -> 42.2 us
    ppermute x7, waiting for transfers between devices: 12.5 us -> 21.6 us  [move(): return lax.ppermute(value, AXES, found)]
    all_to_all x1, blocking collectives: 47.5 us -> 40.3 us  [on_device(): lax.all_to_all(spread, ('far', 'near', 'slc'), split_axis=0, concat_axis=...]
    ppermute x7, starting transfers between devices: 48.1 us -> 42.2 us  [move(): return lax.ppermute(value, AXES, found)]
  transfers between devices with their start and end apart: 7 -> 7, of which waited for: 4 -> 4; matrix products, arithmetic and copies ran while one was open for 0% -> 0% of each run, Pallas kernels for 6% -> 7%
where the time goes in v1:
time: 121 us
  starting transfers between devices  42.2 us (35%)
  blocking collectives  40.3 us (33%)
  waiting for transfers between devices  21.6 us (18%)
  Pallas kernels  14.8 us (12%)
    ppermute x7, starting transfers between devices, move(): return lax.ppermute(value, AXES, found)  42.2 us
    all_to_all x1, blocking collectives, on_device(): lax.all_to_all(spread, ('far', 'near', 'slc'), split_axis=0, concat_axis=...  40.3 us
    ppermute x7, waiting for transfers between devices, move(): return lax.ppermute(value, AXES, found)  21.6 us
    pallas_call x2, Pallas kernels, column_products(): pl.pallas_call(functools.partial(column_kernel, base), out_shape=jax.Shap...  11.4 us
    pallas_call x6, Pallas kernels, join(): pl.pallas_call(join_kernel, out_shape=(out,) * outs, in_specs=[pl.BlockSp...  2.49 us
  transfers between devices with their start and end apart: 7, of which 4 were waited for; matrix products, arithmetic and copies ran while one was open for 0% of the time, Pallas kernels for 7%

profile of v1, /device:TPU:80, one launch (start us, length us, event | category | flops | bytes accessed | tf_op | source)
XLA Modules:
  0.0 120.7 jit_solution(8359779856058088290)
XLA Ops:
  0.0 0.1 pad_add_fusion.1.role_ref
  0.1 0.0 copy-start
  0.1 0.7 copy-done
  0.7 5.7 %column_products.3 = f32[16,64,128]{2,1,0:T(8,128)S(1)} custom-call(s32[18]{0:T(128)S(1)} %copy-done, s32[2]{0:T(128)S(1)} %pad_add_fusion.1.role_ref, s32[32,288]{1,0:T(8,128)} %bits_hbm.3, bf16[18,2,64,128]{3,2,1,0:T(8,128)(2,1)} %bitcast.9, f32[64,128]{1,0:T(8,128)} %bitcast.11, f32[64,128]{1,0:T(8,128)} %bitcast.13), custom_call_target="tpu_custom_call" | custom-call | flops 1207959552 | bytes 1048576 | tf_op jit(solution)/shard_map/column_products/pallas_call | solution.py:159
  6.4 4.8 %collective-permute-start = (f32[16,64,128]{2,1,0:T(8,128)S(1)}, f32[16,64,128]{2,1,0:T(8,128)S(1)}, u32[]{:S(2)}, u32[]{:S(2)}) collective-permute-start(f32[16,64,128]{2,1,0:T(8,128)S(1)} %column_products.3), channel_id=1, source_target_pairs={{0,16},{16,0},{32,48},{48,32},{64,80},{80,64},{96,112},{112,96},{1... | collective-permute-start | bytes 1572872 | tf_op jit(solution)/shard_map/ppermute | solution.py:283
  11.3 0.7 collective-permute-start.4
  12.0 5.7 %column_products.2.kept_ref = f32[16,64,128]{2,1,0:T(8,128)S(1)} custom-call(s32[18]{0:T(128)S(1)} %copy-done, s32[2]{0:T(128)S(1)} %pad_add_fusion.1.role_ref, s32[32,288]{1,0:T(8,128)} %bits_hbm.3, bf16[18,2,64,128]{3,2,1,0:T(8,128)(2,1)} %bitcast.10, f32[64,128]{1,0:T(8,128)} %bitcast.12, f32[64,128]{1,0:T(8,128)} %bitcast.14), custom_call_target="tpu_custom_call" | custom-call | flops 1207959552 | bytes 1048576 | tf_op jit(solution)/shard_map/column_products/pallas_call | solution.py:159
  17.7 0.7 collective-permute-done.received_ref
  18.4 0.6 join.6
  19.0 9.6 %collective-permute-start.1 = (f32[8,64,128]{2,1,0:T(8,128)S(1)}, f32[8,64,128]{2,1,0:T(8,128)S(1)}, u32[]{:S(2)}, u32[]{:S(2)}) collective-permute-start(f32[8,64,128]{2,1,0:T(8,128)S(1)} %get-tuple-element.14), channel_id=1, source_target_pairs={{0,32},{16,48},{32,0},{48,16},{64,96},{80,112},{96,64},{112,80},{1... | collective-permute-start | bytes 786440 | tf_op jit(solution)/shard_map/ppermute | solution.py:283
  28.5 0.0 collective-permute-done.4.received_ref
  28.6 0.6 join.9
  29.1 0.7 collective-permute-start.5
  29.8 7.1 %collective-permute-done.1.received_ref = f32[8,64,128]{2,1,0:T(8,128)S(1)} collective-permute-done((f32[8,64,128]{2,1,0:T(8,128)S(1)}, f32[8,64,128]{2,1,0:T(8,128)S(1)}, u32[]{:S(2)}, u32[]{:S(2)}) %collective-permute-start.1) | collective-permute-done | bytes 262176 | tf_op jit(solution)/shard_map/ppermute | solution.py:283
  37.0 0.4 join.7
  37.3 17.8 %collective-permute-start.2 = (f32[4,64,128]{2,1,0:T(8,128)S(1)}, f32[4,64,128]{2,1,0:T(8,128)S(1)}, u32[]{:S(2)}, u32[]{:S(2)}) collective-permute-start(f32[4,64,128]{2,1,0:T(8,128)S(1)} %get-tuple-element.16), channel_id=1, source_target_pairs={{0,64},{16,80},{32,96},{48,112},{64,0},{80,16},{96,32},{112,48},{1... | collective-permute-start | bytes 393224 | tf_op jit(solution)/shard_map/ppermute | solution.py:283
  55.2 3.3 %collective-permute-done.2.received_ref = f32[4,64,128]{2,1,0:T(8,128)S(1)} collective-permute-done((f32[4,64,128]{2,1,0:T(8,128)S(1)}, f32[4,64,128]{2,1,0:T(8,128)S(1)}, u32[]{:S(2)}, u32[]{:S(2)}) %collective-permute-start.2) | collective-permute-done | bytes 131104 | tf_op jit(solution)/shard_map/ppermute | solution.py:283
  58.5 0.3 join.8
  58.8 8.0 %collective-permute-start.3 = (f32[4,64,128]{2,1,0:T(8,128)S(1)}, f32[4,64,128]{2,1,0:T(8,128)S(1)}, u32[]{:S(2)}, u32[]{:S(2)}) collective-permute-start(f32[4,64,128]{2,1,0:T(8,128)S(1)} %join.8), channel_id=1, source_target_pairs={{0,192},{16,208},{32,224},{48,240},{64,128},{80,144},{96,160},{112... | collective-permute-start | bytes 393224 | tf_op jit(solution)/shard_map/ppermute | solution.py:283
  66.8 0.0 collective-permute-done.5.received_ref
  66.8 0.4 join.10
  67.2 0.7 collective-permute-start.6
  67.9 0.1 pad_add_fusion.role_ref
  67.9 10.4 %collective-permute-done.3.kept_ref = f32[4,64,128]{2,1,0:T(8,128)S(1)} collective-permute-done((f32[4,64,128]{2,1,0:T(8,128)S(1)}, f32[4,64,128]{2,1,0:T(8,128)S(1)}, u32[]{:S(2)}, u32[]{:S(2)}) %collective-permute-start.3) | collective-permute-done | bytes 131104 | tf_op jit(solution)/shard_map/ppermute | solution.py:283
  78.4 0.3 join.11.opened_ref
  78.7 0.0 collective-permute-done.6.received_ref
  78.7 0.9 close.1
  79.7 40.3 %all_to_all.5 = f32[128,2,32]{2,1,0:T(2,128)S(1)} all-to-all(f32[128,2,32]{2,1,0:T(2,128)S(1)} %broadcast_in_dim.18), channel_id=1, replica_groups=mesh['grp'=2,'far'=4,'near'=4,'slc'=8,'bat'=2] {'far','near','slc'}, dimensions={0} | all-to-all | bytes 65536 | tf_op jit(solution)/shard_map/all_to_all | solution.py:302
  120.0 0.7 reduce_sum.9
  (1 shorter events, 0.0 us)
Async XLA Ops:
  0.1 0.7 copy-start
  6.4 12.0 %collective-permute-start = (f32[16,64,128]{2,1,0:T(8,128)S(1)}, f32[16,64,128]{2,1,0:T(8,128)S(1)}, u32[]{:S(2)}, u32[]{:S(2)}) collective-permute-start(f32[16,64,128]{2,1,0:T(8,128)S(1)} %column_products.3), channel_id=1, source_target_pairs={{0,16},{16,0},{32,48},{48,32},{64,80},{80,64},{96,112},{112,96},{1... | collective-permute-start | bytes 1572872 | tf_op jit(solution)/shard_map/ppermute | solution.py:283
  11.3 17.3 %collective-permute-start.4 = (f32[16,64,128]{2,1,0:T(8,128)S(1)}, f32[16,64,128]{2,1,0:T(8,128)S(1)}, u32[]{:S(2)}, u32[]{:S(2)}) collective-permute-start(f32[16,64,128]{2,1,0:T(8,128)S(1)} %column_products.3), channel_id=1, source_target_pairs={{128,144},{144,128},{160,176},{176,160},{192,208},{208,192},{224,2... | collective-permute-start | bytes 1572872 | tf_op jit(solution)/shard_map/ppermute | solution.py:283
  19.0 18.0 %collective-permute-start.1 = (f32[8,64,128]{2,1,0:T(8,128)S(1)}, f32[8,64,128]{2,1,0:T(8,128)S(1)}, u32[]{:S(2)}, u32[]{:S(2)}) collective-permute-start(f32[8,64,128]{2,1,0:T(8,128)S(1)} %get-tuple-element.14), channel_id=1, source_target_pairs={{0,32},{16,48},{32,0},{48,16},{64,96},{80,112},{96,64},{112,80},{1... | collective-permute-start | bytes 786440 | tf_op jit(solution)/shard_map/ppermute | solution.py:283
  29.1 37.6 %collective-permute-start.5 = (f32[8,64,128]{2,1,0:T(8,128)S(1)}, f32[8,64,128]{2,1,0:T(8,128)S(1)}, u32[]{:S(2)}, u32[]{:S(2)}) collective-permute-start(f32[8,64,128]{2,1,0:T(8,128)S(1)} %get-tuple-element.18), channel_id=1, source_target_pairs={{128,160},{144,176},{160,128},{176,144},{192,224},{208,240},{224,1... | collective-permute-start | bytes 786440 | tf_op jit(solution)/shard_map/ppermute | solution.py:283
  37.3 21.1 %collective-permute-start.2 = (f32[4,64,128]{2,1,0:T(8,128)S(1)}, f32[4,64,128]{2,1,0:T(8,128)S(1)}, u32[]{:S(2)}, u32[]{:S(2)}) collective-permute-start(f32[4,64,128]{2,1,0:T(8,128)S(1)} %get-tuple-element.16), channel_id=1, source_target_pairs={{0,64},{16,80},{32,96},{48,112},{64,0},{80,16},{96,32},{112,48},{1... | collective-permute-start | bytes 393224 | tf_op jit(solution)/shard_map/ppermute | solution.py:283
  58.8 19.6 %collective-permute-start.3 = (f32[4,64,128]{2,1,0:T(8,128)S(1)}, f32[4,64,128]{2,1,0:T(8,128)S(1)}, u32[]{:S(2)}, u32[]{:S(2)}) collective-permute-start(f32[4,64,128]{2,1,0:T(8,128)S(1)} %join.8), channel_id=1, source_target_pairs={{0,192},{16,208},{32,224},{48,240},{64,128},{80,144},{96,160},{112... | collective-permute-start | bytes 393224 | tf_op jit(solution)/shard_map/ppermute | solution.py:283
  67.2 11.5 %collective-permute-start.6 = (f32[4,64,128]{2,1,0:T(8,128)S(1)}, f32[4,64,128]{2,1,0:T(8,128)S(1)}, u32[]{:S(2)}, u32[]{:S(2)}) collective-permute-start(f32[4,64,128]{2,1,0:T(8,128)S(1)} %get-tuple-element.20), channel_id=1, source_target_pairs={{128,192},{144,208},{160,224},{176,240},{192,128},{208,144},{224,1... | collective-permute-start | bytes 393224 | tf_op jit(solution)/shard_map/ppermute | solution.py:283
